TPU v7x, 32 devices: a whole 2x2x4 slice. The times are simulated.
32 devices in a mesh: seq: 8 (over z, y), head: 4 (over x, core).
Axes of the slice: x: 2, y: 2, z: 4, core: 2. Of those that a mesh axis runs over, the one named last changes fastest.
Arguments:
- queries: bfloat16 [4096, 12288], P(('seq', 'head')), may hold values from -8 to 8
- latent: bfloat16 [4096, 512], P(('seq', 'head')), may hold values from -6 to 6
- rope_keys: bfloat16 [4096, 64], P(('seq', 'head')), may hold values from -8 to 8
- key_weight: bfloat16 [512, 8192], P('seq', 'head'), may hold values from -0.25 to 0.25
- value_weight: bfloat16 [512, 8192], P('seq', 'head'), may hold values from -0.25 to 0.25
- doc_lengths: int32 [32], replicated, may hold values from 1 to 254, as said below
Outputs:
- attended: bfloat16 [4096, 8192], P(('seq', 'head'))
Inputs may be any that keep to these rules, and one draw needn't show every extreme that they name: `doc_lengths`: the documents lie in order in the pack and their lengths sum to 4096; document 0 starts at position 0 and every other document d starts strictly inside positions d * 128 to (d + 1) * 128 - 1, excluding the first of these; one length is exactly 254.
All inputs are finite; a program needn't handle non-finite values.
Results may differ from a plain program's by a relative error of at most 0.0062.
Values may be sent and summed in bfloat16 or wider, within the bound.
A program may use at most 128 MiB of HBM per device.

v0:
```python
import math
import jax
import jax.numpy as jnp
from jax import lax
from jax.sharding import PartitionSpec as P

NOPE = 128
ROPE = 64
VDIM = 128
lowest_score = -1e30


def shifted(value, axis, steps):
    count = lax.axis_size(axis)
    first, last = (max(0, -steps), min(count, count - steps))
    return lax.ppermute(value, axis, [(source, source + steps) for source in range(first, last)])


def document_of(doc_lengths, first_place, count):
    starts = jnp.cumsum(doc_lengths) - doc_lengths
    places = first_place + jnp.arange(count, dtype=jnp.int32)
    started = (starts[None, :] <= places[:, None]).astype(jnp.int32)
    return jnp.sum(started, axis=1) - 1


def shards(queries, latent, rope_keys, key_weight, value_weight, doc_lengths):
    tok_rows = queries.shape[0]
    groups = lax.axis_size("head")
    group_rows = tok_rows * groups
    local_heads = key_weight.shape[1] // NOPE
    qk_width = NOPE + ROPE
    block_rows = min(512, group_rows)
    score_scale = 1.0 / math.sqrt(qk_width)
    group_latent, group_rope = (
        lax.all_gather(latent, "head", axis=0, tiled=True),
        lax.all_gather(rope_keys, "head", axis=0, tiled=True),
    )
    by_heads = queries.reshape(tok_rows, groups, local_heads * qk_width)
    my_queries = lax.all_to_all(by_heads, "head", split_axis=1, concat_axis=0, tiled=True)
    my_queries = my_queries.reshape(group_rows, local_heads, qk_width)
    earlier_latent, earlier_rope = shifted((group_latent, group_rope), "seq", 1)
    latent_rows = jnp.concatenate([earlier_latent, group_latent], axis=0)
    key_sums = jnp.dot(
        latent_rows,
        lax.all_gather(key_weight, "seq", axis=0, tiled=True),
        preferred_element_type=jnp.float32,
    )
    value_sums = jnp.dot(
        latent_rows,
        lax.all_gather(value_weight, "seq", axis=0, tiled=True),
        preferred_element_type=jnp.float32,
    )
    keys_all = key_sums.astype(jnp.bfloat16)
    values_all = value_sums.astype(jnp.bfloat16)
    rope_all = jnp.concatenate([earlier_rope, group_rope], axis=0)
    first_place = lax.axis_index("seq") * group_rows - group_rows
    key_docs = document_of(doc_lengths, first_place, 2 * group_rows)
    key_blocks = group_rows // block_rows + 1

    def one_block(q_index):
        q_start = q_index * block_rows
        q_block = lax.dynamic_slice_in_dim(my_queries, q_start, block_rows, 0)
        q_nope = q_block[:, :, :NOPE]
        q_rope = q_block[:, :, NOPE:]
        q_docs = lax.dynamic_slice_in_dim(key_docs, group_rows + q_start, block_rows, 0)
        q_places = group_rows + q_start + jnp.arange(block_rows, dtype=jnp.int32)

        def attend(state_now, k_start):
            row_peak, row_sum, weighted = state_now
            k_nope = lax.dynamic_slice_in_dim(keys_all, k_start, block_rows, 0).reshape(
                block_rows, local_heads, NOPE
            )
            k_rope = lax.dynamic_slice_in_dim(rope_all, k_start, block_rows, 0)
            k_values = lax.dynamic_slice_in_dim(values_all, k_start, block_rows, 0).reshape(
                block_rows, local_heads, VDIM
            )
            k_docs = lax.dynamic_slice_in_dim(key_docs, k_start, block_rows, 0)
            k_places = k_start + jnp.arange(block_rows, dtype=jnp.int32)
            scores = jnp.einsum("ihd,jhd->hij", q_nope, k_nope, preferred_element_type=jnp.float32)
            scores = (
                scores
                + jnp.einsum("ihd,jd->hij", q_rope, k_rope, preferred_element_type=jnp.float32)
            ) * score_scale
            allowed = (q_docs[:, None] == k_docs[None, :]) & (
                k_places[None, :] <= q_places[:, None]
            )
            scores = jnp.where(allowed[None, :, :], scores, -jnp.inf)
            new_peak = jnp.maximum(row_peak, jnp.max(scores, axis=2))
            expo = jnp.exp(scores - new_peak[:, :, None])
            rescale = jnp.exp(row_peak - new_peak)
            row_sum = row_sum * rescale + jnp.sum(expo, axis=2)
            rounded = expo.astype(jnp.bfloat16)
            weighted = weighted * jnp.transpose(rescale)[:, :, None] + jnp.einsum(
                "hij,jhd->ihd", rounded, k_values, preferred_element_type=jnp.float32
            )
            return (new_peak, row_sum, weighted)

        def visit(k_index, state_now):
            k_start = (q_index + k_index) * block_rows
            return attend(state_now, k_start)

        start_state = (
            jnp.full((local_heads, block_rows), lowest_score, jnp.float32),
            jnp.zeros((local_heads, block_rows), jnp.float32),
            jnp.zeros((block_rows, local_heads, VDIM), jnp.float32),
        )
        row_peak, row_sum, weighted = lax.fori_loop(0, key_blocks, visit, start_state)
        mixed = weighted / jnp.transpose(row_sum)[:, :, None]
        return mixed.reshape(block_rows, local_heads * VDIM).astype(jnp.bfloat16)

    attended = lax.map(one_block, jnp.arange(group_rows // block_rows, dtype=jnp.int32))
    attended = attended.reshape(group_rows, local_heads * VDIM)
    return lax.all_to_all(attended, "head", split_axis=0, concat_axis=1, tiled=True)


def solution(mesh):
    placed = (
        P(("seq", "head"), None),
        P(("seq", "head"), None),
        P(("seq", "head"), None),
        P("seq", "head"),
        P("seq", "head"),
        P(),
    )
    return jax.shard_map(
        shards, mesh=mesh, in_specs=placed, out_specs=P(("seq", "head"), None), check_vma=False
    )
```

profile of v0, /device:TPU:24, one launch (start us, length us, event | category | flops | bytes accessed | tf_op | source)
XLA Modules:
  0.0 263.6 jit_solution(16397362102744043481)
XLA Ops:
  6.5 0.7 all-gather.5.cloned.1.call-update
  7.3 0.0 all-gather.3.cloned.1.call-start
  7.3 0.7 all-gather.3.cloned.1.call-update
  8.0 4.7 %copy.43 = bf16[128,12288]{0,1:T(8,128)(2,1)} copy(bf16[128,12288]{1,0:T(8,128)(2,1)} %param.8) | data formatting | bytes 6291456 | tf_op args[0]
  12.7 3.8 %all-to-all-start = ((bf16[128,4,3072]{0,2,1:T(8,128)(2,1)}), bf16[128,4,3072]{0,2,1:T(8,128)(2,1)S(1)}, u32[]{:S(2)}, u32[]{:S(2)}) async-start(bf16[128,4,3072]{0,2,1:T(8,128)(2,1)} %bitcast.61), calls=%async_computation | async-start | bytes 6291456 | tf_op jit(solution)/shard_map/all_to_all | solution.py:39
  16.5 41.0 %all_gather.12 = bf16[512,512]{1,0:T(8,128)(2,1)} all-gather(bf16[128,512]{1,0:T(8,128)(2,1)S(1)} %copy-done), channel_id=1, replica_groups=mesh['seq'=8,'head'=4] {'head'}, dimensions={0}, use_global_device_ids=true | all-gather | bytes 655360 | tf_op jit(solution)/shard_map/all_gather | solution.py:35
  57.5 3.4 %collective-permute-start = (bf16[512,512]{1,0:T(8,128)(2,1)}, bf16[512,512]{1,0:T(8,128)(2,1)}, u32[]{:S(2)}, u32[]{:S(2)}) collective-permute-start(bf16[512,512]{1,0:T(8,128)(2,1)} %all_gather.12), channel_id=1, source_target_pairs={{0,4},{4,8},{8,12},{12,16},{16,20},{20,24},{24,28},{1,5},{5,9},{9,... | collective-permute-start | bytes 1572872 | tf_op jit(solution)/shard_map/ppermute | solution.py:16
  60.9 5.3 %all_gather.14 = bf16[512,64]{0,1:T(8,128)(2,1)S(1)} all-gather(bf16[128,64]{0,1:T(8,128)(2,1)S(1)} %copy-done.1), channel_id=1, replica_groups=mesh['seq'=8,'head'=4] {'head'}, dimensions={0}, use_global_device_ids=true | all-gather | bytes 81920 | tf_op jit(solution)/shard_map/all_gather | solution.py:36
  66.2 1.9 collective-permute-start.1
  68.1 0.1 copy.42
  68.2 0.1 reduce-window.9
  68.3 0.1 reduce
  68.4 0.1 convert_reduce_fusion
  68.6 15.9 %collective-permute-done.1 = bf16[512,64]{0,1:T(8,128)(2,1)S(1)} collective-permute-done((bf16[512,64]{0,1:T(8,128)(2,1)S(1)}, bf16[512,64]{0,1:T(8,128)(2,1)S(1)}, u32[]{:S(2)}, u32[]{:S(2)}) %collective-permute-start.1) | collective-permute-done | bytes 65568 | tf_op jit(solution)/shard_map/ppermute | solution.py:16
  84.5 1.9 constant_dynamic-update-slice_fusion.1
  86.4 1.9 constant_dynamic-update-slice_fusion
  88.3 15.6 %copy.44 = bf16[4,128,1,3072]{1,0,3,2:T(4,128)(2,1)} copy(bf16[4,128,1,3072]{1,3,0,2:T(8,128)(2,1)S(1)} %bitcast.60) | data formatting | bytes 6291456 | tf_op jit(solution)/shard_map/all_to_all | solution.py:39
  103.9 4.0 %reshape.132 = bf16[512,16,192]{0,2,1:T(8,128)(2,1)S(1)} reshape(bf16[4,128,1,3072]{1,0,3,2:T(4,128)(2,1)} %copy.44) | data formatting | bytes 6291456 | tf_op jit(solution)/shard_map/reshape | solution.py:40
  107.9 1.5 slice.11
  109.4 1.1 slice.12
  110.5 3.9 %copy.46 = bf16[512,16,128]{2,0,1:T(8,128)(2,1)} copy(bf16[512,16,128]{0,2,1:T(8,128)(2,1)} %slice.11) | data formatting | bytes 4194304
  114.4 6.2 %convolution_convert_fusion = bf16[1024,2048]{1,0:T(8,128)(2,1)} fusion(bf16[1024,512]{1,0:T(8,128)(2,1)} %constant_dynamic-update-slice_fusion, bf16[512,2048]{1,0:T(8,128)(2,1)} %all-gather.5.cloned.1.call-done), kind=kOutput, calls=%fused_computation.25 | convolution fusion | flops 2149580800 | bytes 7340032 | tf_op jit(solution)/shard_map/dot_general | solution.py:48
  120.6 6.2 %convolution_convert_fusion.1 = bf16[1024,2048]{1,0:T(8,128)(2,1)} fusion(bf16[1024,512]{1,0:T(8,128)(2,1)} %constant_dynamic-update-slice_fusion, bf16[512,2048]{1,0:T(8,128)(2,1)} %all-gather.3.cloned.1.call-done), kind=kOutput, calls=%fused_computation.26 | convolution fusion | flops 2149580800 | bytes 7340032 | tf_op jit(solution)/shard_map/dot_general | solution.py:43
  126.8 87.3 %while.27 = (s32[]{:T(128)}, f32[16,512]{1,0:T(8,128)S(1)}, f32[16,512]{1,0:T(8,128)S(1)}, f32[512,16,128]{0,2,1:T(8,128)}, s32[512]{0:T(512)S(1)}, /*index=5*/s...) while((s32[]{:T(128)}, f32[16,512]{1,0:T(8,128)S(1)}, ...), condition=%wide.region_5.6_spmd.clone, body=%wide.region_2.5_spmd.clone.sunk | while | flops 2721891328 | bytes 117522640 | solution.py:107
  126.8 0.1 dynamic_slice.63
  126.9 0.3 compare_and_fusion.2
  127.2 4.8 %constant_dynamic-slice_fusion.3 = (bf16[512,2048]{1,0:T(8,128)(2,1)}, bf16[512,2048]{1,0:T(8,128)(2,1)}) fusion(bf16[1024,2048]{1,0:T(8,128)(2,1)} %get-tuple-element.540, s32[]{:T(128)S(6)} %select_n.30, bf16[1024,2048]{1,0:T(8,128)(2,1)} %get-tuple-element.536), kind=kLoop, calls=%fused_computation.21.clone.1 | loop fusion | bytes 8388612 | tf_op jit(solution)/shard_map/while/body/eval_jaxpr/while/body/eval_jaxpr/dynamic_slice | solution.py:74
  132.1 2.9 %copy.58 = bf16[512,2048]{0,1:T(8,128)(2,1)S(1)} copy(bf16[512,2048]{1,0:T(8,128)(2,1)} %get-tuple-element.492) | data formatting | bytes 4194304 | tf_op jit(solution)/shard_map/while/body/eval_jaxpr/while/body/eval_jaxpr/dynamic_slice | solution.py:70
  134.9 4.0 %fusion.41 = f32[16,512,512]{2,1,0:T(8,128)S(1)} fusion(bf16[512,16,128]{0,2,1:T(8,128)(2,1)S(1)} %bitcast.59, bf16[512,16,128]{2,0,1:T(8,128)(2,1)} %get-tuple-element.537), kind=kOutput, calls=%fused_computation.34.clone.1 | convolution fusion | flops 1073741824 | bytes 20971520 | tf_op jit(solution)/shard_map/while/body/eval_jaxpr/while/body/eval_jaxpr/ihd,jhd->hij/dot_general | solution.py:79
  138.9 9.0 %fusion.42 = (f32[16,512]{1,0:T(8,128)S(1)}, f32[16,512,512]{1,2,0:T(8,128)}) fusion(bf16[512,16,64]{0,2,1:T(8,128)(2,1)} %get-tuple-element.539, bf16[1024,64]{0,1:T(8,128)(2,1)S(1)} %get-tuple-element.538, s32[]{:T(128)S(6)} %select_n.30, f32[16,512,512]{2,1,0:T(8,128)S(1)} %fusion.41, pred[512,512]{0,1:T(8,128)(4,1)S(1)} %compare_and_fusion.2), kind=kOutput, calls=%fused_computation.33.clone.1 | convolution fusion | flops 553639936 | bytes 34963460 | tf_op jit(solution)/shard_map/while/body/eval_jaxpr/while/body/eval_jaxpr/ihd,jd->hij/dot_general | solution.py:82
  147.9 2.9 %copy.59 = bf16[512,2048]{0,1:T(8,128)(2,1)S(1)} copy(bf16[512,2048]{1,0:T(8,128)(2,1)} %get-tuple-element.498) | data formatting | bytes 4194304 | tf_op jit(solution)/shard_map/while/body/eval_jaxpr/while/body/eval_jaxpr/dynamic_slice | solution.py:74
  150.8 10.8 %bitcast_add_fusion.3 = f32[512,16,128]{0,2,1:T(8,128)} fusion(f32[512,16,128]{0,2,1:T(8,128)} %get-tuple-element.518, bf16[512,16,128]{0,2,1:T(8,128)(2,1)S(1)} %bitcast.58, f32[16,512,512]{1,2,0:T(8,128)} %get-tuple-element.497, f32[16,512]{1,0:T(8,128)S(1)} %get-tuple-element.531, f32[512,16]{0,1:T(8,128)S(1)} %get-tuple-element.499, pred[]{:T(512)S(6)} %compare.3), kind=kOutput, calls=%fused_computation.9.clone.1 | convolution fusion | flops 1085276160 | bytes 27328512 | tf_op jit(solution)/shard_map/while/body/eval_jaxpr/while/body/eval_jaxpr/hij,jhd->ihd/dot_general | solution.py:93
  161.6 8.3 %fusion.44 = f32[16,512]{1,0:T(8,128)S(1)} fusion(f32[16,512,512]{1,2,0:T(8,128)} %get-tuple-element.497, f32[16,512]{1,0:T(8,128)S(1)} %get-tuple-element.531), kind=kLoop, calls=%fused_computation.6.clone.1 | loop fusion | flops 8380416 | bytes 16842752 | tf_op jit(solution)/shard_map/while/body/eval_jaxpr/while/body/eval_jaxpr/reduce_sum | solution.py:91
  169.9 0.1 dynamic_slice.63
  170.0 0.3 compare_and_fusion.2
  170.3 4.8 %constant_dynamic-slice_fusion.3 = (bf16[512,2048]{1,0:T(8,128)(2,1)}, bf16[512,2048]{1,0:T(8,128)(2,1)}) fusion(bf16[1024,2048]{1,0:T(8,128)(2,1)} %get-tuple-element.540, s32[]{:T(128)S(6)} %select_n.30, bf16[1024,2048]{1,0:T(8,128)(2,1)} %get-tuple-element.536), kind=kLoop, calls=%fused_computation.21.clone.1 | loop fusion | bytes 8388612 | tf_op jit(solution)/shard_map/while/body/eval_jaxpr/while/body/eval_jaxpr/dynamic_slice | solution.py:74
  175.1 2.9 %copy.58 = bf16[512,2048]{0,1:T(8,128)(2,1)S(1)} copy(bf16[512,2048]{1,0:T(8,128)(2,1)} %get-tuple-element.492) | data formatting | bytes 4194304 | tf_op jit(solution)/shard_map/while/body/eval_jaxpr/while/body/eval_jaxpr/dynamic_slice | solution.py:70
  178.0 4.0 %fusion.41 = f32[16,512,512]{2,1,0:T(8,128)S(1)} fusion(bf16[512,16,128]{0,2,1:T(8,128)(2,1)S(1)} %bitcast.59, bf16[512,16,128]{2,0,1:T(8,128)(2,1)} %get-tuple-element.537), kind=kOutput, calls=%fused_computation.34.clone.1 | convolution fusion | flops 1073741824 | bytes 20971520 | tf_op jit(solution)/shard_map/while/body/eval_jaxpr/while/body/eval_jaxpr/ihd,jhd->hij/dot_general | solution.py:79
  182.0 9.0 %fusion.42 = (f32[16,512]{1,0:T(8,128)S(1)}, f32[16,512,512]{1,2,0:T(8,128)}) fusion(bf16[512,16,64]{0,2,1:T(8,128)(2,1)} %get-tuple-element.539, bf16[1024,64]{0,1:T(8,128)(2,1)S(1)} %get-tuple-element.538, s32[]{:T(128)S(6)} %select_n.30, f32[16,512,512]{2,1,0:T(8,128)S(1)} %fusion.41, pred[512,512]{0,1:T(8,128)(4,1)S(1)} %compare_and_fusion.2), kind=kOutput, calls=%fused_computation.33.clone.1 | convolution fusion | flops 553639936 | bytes 34963460 | tf_op jit(solution)/shard_map/while/body/eval_jaxpr/while/body/eval_jaxpr/ihd,jd->hij/dot_general | solution.py:82
  190.9 2.9 %copy.59 = bf16[512,2048]{0,1:T(8,128)(2,1)S(1)} copy(bf16[512,2048]{1,0:T(8,128)(2,1)} %get-tuple-element.498) | data formatting | bytes 4194304 | tf_op jit(solution)/shard_map/while/body/eval_jaxpr/while/body/eval_jaxpr/dynamic_slice | solution.py:74
  193.8 12.0 %bitcast_add_fusion.3 = f32[512,16,128]{0,2,1:T(8,128)} fusion(f32[512,16,128]{0,2,1:T(8,128)} %get-tuple-element.518, bf16[512,16,128]{0,2,1:T(8,128)(2,1)S(1)} %bitcast.58, f32[16,512,512]{1,2,0:T(8,128)} %get-tuple-element.497, f32[16,512]{1,0:T(8,128)S(1)} %get-tuple-element.531, f32[512,16]{0,1:T(8,128)S(1)} %get-tuple-element.499, pred[]{:T(512)S(6)} %compare.3), kind=kOutput, calls=%fused_computation.9.clone.1 | convolution fusion | flops 1085276160 | bytes 27328512 | tf_op jit(solution)/shard_map/while/body/eval_jaxpr/while/body/eval_jaxpr/hij,jhd->ihd/dot_general | solution.py:93
  205.8 8.3 %fusion.44 = f32[16,512]{1,0:T(8,128)S(1)} fusion(f32[16,512,512]{1,2,0:T(8,128)} %get-tuple-element.497, f32[16,512]{1,0:T(8,128)S(1)} %get-tuple-element.531), kind=kLoop, calls=%fused_computation.6.clone.1 | loop fusion | flops 8380416 | bytes 16842752 | tf_op jit(solution)/shard_map/while/body/eval_jaxpr/while/body/eval_jaxpr/reduce_sum | solution.py:91
  214.1 2.8 %divide_convert_fusion = bf16[512,16,128]{0,2,1:T(8,128)(2,1)S(1)} fusion(f32[512,16,128]{0,2,1:T(8,128)} %get-tuple-element.292, f32[512,16]{0,1:T(8,128)S(1)} %bitcast.63), kind=kLoop, calls=%fused_computation.24 | loop fusion | flops 2097152 | bytes 6324224 | tf_op jit(solution)/shard_map/while/body/eval_jaxpr/convert_element_type | solution.py:109
  216.9 2.0 reshape.136
  219.0 3.0 %copy.53 = bf16[4,128,2048]{2,1,0:T(8,128)(2,1)S(1)} copy(bf16[4,128,2048]{1,0,2:T(4,128)(2,1)} %reshape.136) | data formatting | bytes 4194304 | tf_op jit(solution)/shard_map/while/body/eval_jaxpr/convert_element_type | solution.py:109
  221.9 28.9 %all_to_all.31 = bf16[4,128,2048]{2,1,0:T(8,128)(2,1)} all-to-all(bf16[4,128,2048]{2,1,0:T(8,128)(2,1)S(1)} %copy.53), channel_id=1, replica_groups=mesh['seq'=8,'head'=4] {'head'}, dimensions={0} | all-to-all | bytes 4194304 | tf_op jit(solution)/shard_map/all_to_all | solution.py:113
  250.8 3.0 %copy.49 = bf16[4,128,2048]{1,2,0:T(8,128)(2,1)S(1)} copy(bf16[4,128,2048]{2,1,0:T(8,128)(2,1)} %all_to_all.31) | data formatting | bytes 4194304 | tf_op jit(solution)/shard_map/all_to_all | solution.py:113
  253.9 2.9 %copy.50 = bf16[128,8192]{1,0:T(8,128)(2,1)} copy(bf16[128,8192]{0,1:T(8,128)(2,1)S(1)} %bitcast.62) | data formatting | bytes 4194304 | tf_op jit(solution)/shard_map/all_to_all | solution.py:113
  (27 shorter events, 0.1 us)
Async XLA Ops:
  6.5 107.9 %all-gather.5.cloned.1.call-start = ((), (), s32[]{:S(2)}) async-start(), calls=%async_computation.3 | async-start | bytes 2359296 | tf_op jit(solution)/shard_map/all_gather | solution.py:50
  7.3 113.4 %all-gather.3.cloned.1.call-start = ((), (), s32[]{:S(2)}) async-start(), calls=%async_computation.2 | async-start | bytes 2359296 | tf_op jit(solution)/shard_map/all_gather | solution.py:45
  12.7 3.9 %copy-start = (bf16[128,512]{1,0:T(8,128)(2,1)S(1)}, bf16[128,512]{1,0:T(8,128)(2,1)}, u32[]{:S(2)}) copy-start(bf16[128,512]{1,0:T(8,128)(2,1)} %param.9) | copy-start | bytes 393220
  12.7 48.3 %copy-start.1 = (bf16[128,64]{0,1:T(8,128)(2,1)S(1)}, bf16[128,64]{0,1:T(8,128)(2,1)}, u32[]{:S(2)}) copy-start(bf16[128,64]{0,1:T(8,128)(2,1)} %param.10) | copy-start | bytes 49156
  12.7 55.5 %copy-start.2 = (s32[32]{0:T(128)S(1)}, s32[32]{0:T(128)}, u32[]{:S(2)}) copy-start(s32[32]{0:T(128)} %param.13) | copy-start | bytes 388
  12.7 75.6 %all-to-all-start = ((bf16[128,4,3072]{0,2,1:T(8,128)(2,1)}), bf16[128,4,3072]{0,2,1:T(8,128)(2,1)S(1)}, u32[]{:S(2)}, u32[]{:S(2)}) async-start(bf16[128,4,3072]{0,2,1:T(8,128)(2,1)} %bitcast.61), calls=%async_computation | async-start | bytes 6291456 | tf_op jit(solution)/shard_map/all_to_all | solution.py:39
  57.5 27.0 %collective-permute-start = (bf16[512,512]{1,0:T(8,128)(2,1)}, bf16[512,512]{1,0:T(8,128)(2,1)}, u32[]{:S(2)}, u32[]{:S(2)}) collective-permute-start(bf16[512,512]{1,0:T(8,128)(2,1)} %all_gather.12), channel_id=1, source_target_pairs={{0,4},{4,8},{8,12},{12,16},{16,20},{20,24},{24,28},{1,5},{5,9},{9,... | collective-permute-start | bytes 1572872 | tf_op jit(solution)/shard_map/ppermute | solution.py:16
  66.2 18.3 %collective-permute-start.1 = (bf16[512,64]{0,1:T(8,128)(2,1)S(1)}, bf16[512,64]{0,1:T(8,128)(2,1)S(1)}, u32[]{:S(2)}, u32[]{:S(2)}) collective-permute-start(bf16[512,64]{0,1:T(8,128)(2,1)S(1)} %all_gather.14), channel_id=1, source_target_pairs={{0,4},{4,8},{8,12},{12,16},{16,20},{20,24},{24,28},{1,5},{5,9},{9,... | collective-permute-start | bytes 196616 | tf_op jit(solution)/shard_map/ppermute | solution.py:16
Sparse Core Ops, SparseCore 0:
  9.5 48.5 all-gather.4
  60.2 50.0 all-gather.2
where the time goes:
time: 265 us; the launch traced here: 264 us
  blocking collectives  75.1 us (28%)
  local copies, waits for them, and re-layouts  66.8 us (25%)
  matrix products  61.1 us (23%)
  other arithmetic  20.3 us (8%)
  waiting for transfers between devices  17.4 us (7%)
  between operations  13.6 us (5%)
  starting transfers between devices  9.2 us (3%)
    all_gather x1, blocking collectives, shards(): lax.all_gather(latent, 'head', axis=0, tiled=True)  41 us
    all_to_all x1, blocking collectives, shards(): lax.all_to_all(attended, 'head', split_axis=0, concat_axis=1, tiled=True)  28.9 us
    dot_general x2, matrix products, attend(): jnp.einsum('hij,jhd->ihd', rounded, k_values, preferred_element_type=jnp....  22.8 us
    dot_general x2, matrix products, attend(): jnp.einsum('ihd,jd->hij', q_rope, k_rope, preferred_element_type=jnp.floa...  18 us
    reduce_sum x2, other arithmetic, attend(): row_sum = row_sum * rescale + jnp.sum(expo, axis=2)  16.5 us
    ppermute x2, waiting for transfers between devices, shifted(): lax.ppermute(value, axis, [(source, source + steps) for source in range(f...  15.9 us
    all_to_all x1, local copies, waits for them, and re-layouts, shards(): lax.all_to_all(by_heads, 'head', split_axis=1, concat_axis=0, tiled=True)  15.6 us
    dynamic_slice x4, local copies, waits for them, and re-layouts, attend(): lax.dynamic_slice_in_dim(values_all, k_start, block_rows, 0)  15.4 us
  transfers between devices with their start and end apart: 5, of which 1 were waited for; matrix products, arithmetic and copies ran while one was open for 16% of the time, Pallas kernels for 0%

commit v1 on v0

--- a/solution.py
+++ b/solution.py
@@ -8,6 +8,27 @@
 ROPE = 64
 VDIM = 128
 lowest_score = -1e30
+
+
+def slabs_proceed(w_in, dim_k):
+    t_next = list(w_in.shape[1:])
+    t_next[dim_k] *= w_in.shape[0]
+    long_array = jnp.moveaxis(w_in, 0, dim_k).reshape(t_next)
+    return long_array
+
+
+def lift_series(body, comm_axis, array_axis):
+    cores_n = lax.axis_size(comm_axis)
+    store = []
+    for p in range(cores_n):
+        store.append((p, (p + 1) % cores_n))
+    pages = [body]
+    while len(pages) < cores_n:
+        pages.append(lax.ppermute(pages[-1], comm_axis, store))
+    piece_now = lax.axis_index(comm_axis)
+    pages = jnp.stack(pages, axis=0)[(piece_now - jnp.arange(cores_n)) % cores_n]
+    p_next = slabs_proceed(pages, array_axis)
+    return p_next
 
 
 def shifted(value, axis, steps):
@@ -32,7 +53,7 @@
     block_rows = min(512, group_rows)
     score_scale = 1.0 / math.sqrt(qk_width)
     group_latent, group_rope = (
-        lax.all_gather(latent, "head", axis=0, tiled=True),
+        lift_series(latent, "head", 0),
         lax.all_gather(rope_keys, "head", axis=0, tiled=True),
     )
     by_heads = queries.reshape(tok_rows, groups, local_heads * qk_width)

time: 265 us -> 258 us (0.974); the launches traced: 264 us -> 254 us
  blocking collectives: 75.1 us -> 34.4 us
  waiting for transfers between devices: 17.4 us -> 46.3 us
    ppermute x0 -> x3, waiting for transfers between devices: none -> 42.1 us  [lift_series(): pages.append(lax.ppermute(pages[-1], comm_axis, store))]
    all_gather x1 -> x0, blocking collectives: 41 us -> none  [shards(): lax.all_gather(latent, 'head', axis=0, tiled=True)]
    ppermute x2, waiting for transfers between devices: 15.9 us -> 0.01 us  [shifted(): lax.ppermute(value, axis, [(source, source + steps) for source in range(f...]
    all_gather x1, waiting for transfers between devices: 0.01 us -> 2.71 us  [shards(): lax.all_gather(key_weight, 'seq', axis=0, tiled=True)]
    unnamed x9 -> x10, local copies, waits for them, and re-layouts: 10.5 us -> 8.6 us
  transfers between devices with their start and end apart: 5 -> 8, of which waited for: 1 -> 3; matrix products, arithmetic and copies ran while one was open for 16% -> 17% of each run, Pallas kernels for 0% -> 0%
where the time goes in v1:
time: 258 us; the launch traced here: 254 us
  local copies, waits for them, and re-layouts  65.6 us (25%)
  matrix products  60.9 us (24%)
  waiting for transfers between devices  46.3 us (18%)
  blocking collectives  34.4 us (13%)
  other arithmetic  22.9 us (9%)
  between operations  13.6 us (5%)
  starting transfers between devices  9.79 us (4%)
    ppermute x3, waiting for transfers between devices, lift_series(): pages.append(lax.ppermute(pages[-1], comm_axis, store))  42.1 us
    all_to_all x1, blocking collectives, shards(): lax.all_to_all(attended, 'head', split_axis=0, concat_axis=1, tiled=True)  28.9 us
    dot_general x2, matrix products, attend(): jnp.einsum('hij,jhd->ihd', rounded, k_values, preferred_element_type=jnp....  22.8 us
    dot_general x2, matrix products, attend(): jnp.einsum('ihd,jd->hij', q_rope, k_rope, preferred_element_type=jnp.floa...  17.9 us
    reduce_sum x2, other arithmetic, attend(): row_sum = row_sum * rescale + jnp.sum(expo, axis=2)  16.5 us
    all_to_all x1, local copies, waits for them, and re-layouts, shards(): lax.all_to_all(by_heads, 'head', split_axis=1, concat_axis=0, tiled=True)  15.6 us
    dynamic_slice x4, local copies, waits for them, and re-layouts, attend(): lax.dynamic_slice_in_dim(values_all, k_start, block_rows, 0)  15.4 us
    unnamed x10, local copies, waits for them, and re-layouts  8.6 us
  transfers between devices with their start and end apart: 8, of which 3 were waited for; matrix products, arithmetic and copies ran while one was open for 17% of the time, Pallas kernels for 0%

profile of v1, /device:TPU:24, one launch (start us, length us, event | category | flops | bytes accessed | tf_op | source)
XLA Modules:
  0.0 253.6 jit_solution(2428251457031737175)
XLA Ops:
  6.5 0.7 all-gather.5.cloned.1.call-update
  7.3 0.7 all-gather.3.cloned.1.call-update
  8.0 4.6 %copy.43 = bf16[128,12288]{0,1:T(8,128)(2,1)} copy(bf16[128,12288]{1,0:T(8,128)(2,1)} %param.8) | data formatting | bytes 6291456 | tf_op args[0]
  12.7 3.8 %all-to-all-start = ((bf16[128,4,3072]{0,2,1:T(8,128)(2,1)}), bf16[128,4,3072]{0,2,1:T(8,128)(2,1)S(1)}, u32[]{:S(2)}, u32[]{:S(2)}) async-start(bf16[128,4,3072]{0,2,1:T(8,128)(2,1)} %bitcast.66), calls=%async_computation | async-start | bytes 6291456 | tf_op jit(solution)/shard_map/all_to_all | solution.py:60
  16.5 0.5 collective-permute-start
  17.0 37.8 %collective-permute-done = bf16[128,512]{1,0:T(8,128)(2,1)S(1)} collective-permute-done((bf16[128,512]{1,0:T(8,128)(2,1)S(1)}, bf16[128,512]{1,0:T(8,128)(2,1)S(1)}, u32[]{:S(2)}, u32[]{:S(2)}) %collective-permute-start) | collective-permute-done | bytes 131104 | tf_op jit(solution)/shard_map/ppermute | solution.py:27
  54.8 5.5 %all_gather.10 = bf16[512,64]{0,1:T(8,128)(2,1)S(1)} all-gather(bf16[128,64]{0,1:T(8,128)(2,1)S(1)} %copy-done.2), channel_id=1, replica_groups=mesh['seq'=8,'head'=4] {'head'}, dimensions={0}, use_global_device_ids=true | all-gather | bytes 81920 | tf_op jit(solution)/shard_map/all_gather | solution.py:57
  60.3 3.4 %collective-permute-start.4 = (bf16[512,64]{0,1:T(8,128)(2,1)S(1)}, bf16[512,64]{0,1:T(8,128)(2,1)}, u32[]{:S(2)}, u32[]{:S(2)}) collective-permute-start(bf16[512,64]{0,1:T(8,128)(2,1)S(1)} %all_gather.10), channel_id=1, source_target_pairs={{0,4},{4,8},{8,12},{12,16},{16,20},{20,24},{24,28},{1,5},{5,9},{9,... | collective-permute-start | bytes 196616 | tf_op jit(solution)/shard_map/ppermute | solution.py:37
  63.7 0.1 collective-permute-start.2
  63.9 0.1 copy.42
  64.0 0.1 reduce
  64.1 4.3 %collective-permute-done.2 = bf16[128,512]{1,0:T(8,128)(2,1)} collective-permute-done((bf16[128,512]{1,0:T(8,128)(2,1)}, bf16[128,512]{1,0:T(8,128)(2,1)}, u32[]{:S(2)}, u32[]{:S(2)}) %collective-permute-start.2) | collective-permute-done | bytes 131104 | tf_op jit(solution)/shard_map/ppermute | solution.py:27
  68.5 1.8 pad_maximum_fusion.3
  70.3 2.4 gather_fusion
  72.7 1.9 collective-permute-start.3
  74.7 0.1 convert_reduce_fusion
  74.8 0.8 pad_maximum_fusion.4
  75.7 15.6 %copy.44 = bf16[4,128,1,3072]{1,0,3,2:T(4,128)(2,1)} copy(bf16[4,128,1,3072]{1,3,0,2:T(8,128)(2,1)S(1)} %bitcast.65) | data formatting | bytes 6291456 | tf_op jit(solution)/shard_map/all_to_all | solution.py:60
  91.3 4.0 %reshape.185 = bf16[512,16,192]{0,2,1:T(8,128)(2,1)S(1)} reshape(bf16[4,128,1,3072]{1,0,3,2:T(4,128)(2,1)} %copy.44) | data formatting | bytes 6291456 | tf_op jit(solution)/shard_map/reshape | solution.py:61
  95.3 1.5 slice.13
  96.9 1.1 slice.14
  97.9 3.9 %copy.46 = bf16[512,16,128]{2,0,1:T(8,128)(2,1)} copy(bf16[512,16,128]{0,2,1:T(8,128)(2,1)} %slice.13) | data formatting | bytes 4194304
  101.9 6.1 %convolution_convert_fusion = bf16[1024,2048]{1,0:T(8,128)(2,1)} fusion(bf16[512,2048]{1,0:T(8,128)(2,1)} %all-gather.5.cloned.1.call-done, bf16[512,512]{1,0:T(8,128)(2,1)S(1)} %bitcast.70, bf16[512,512]{1,0:T(8,128)(2,1)} %collective-permute-done.3), kind=kOutput, calls=%fused_computation.26 | convolution fusion | flops 2151677952 | bytes 7340032 | tf_op jit(solution)/shard_map/dot_general | solution.py:69
  108.0 2.7 %all-gather.3.cloned.1.call-done = bf16[512,2048]{1,0:T(8,128)(2,1)} async-done(((bf16[64,2048]{1,0:T(8,128)(2,1)}), bf16[512,2048]{1,0:T(8,128)(2,1)}) %all-gather.3.cloned.1.call-update) | async-done | bytes 2097168 | tf_op jit(solution)/shard_map/all_gather | solution.py:66
  110.7 6.1 %convolution_convert_fusion.1 = bf16[1024,2048]{1,0:T(8,128)(2,1)} fusion(bf16[512,2048]{1,0:T(8,128)(2,1)} %all-gather.3.cloned.1.call-done, bf16[512,512]{1,0:T(8,128)(2,1)S(1)} %bitcast.71, bf16[512,512]{1,0:T(8,128)(2,1)} %collective-permute-done.3), kind=kOutput, calls=%fused_computation.27 | convolution fusion | flops 2151677952 | bytes 7340032 | tf_op jit(solution)/shard_map/dot_general | solution.py:64
  116.8 87.3 %while.27 = (s32[]{:T(128)}, f32[16,512]{1,0:T(8,128)S(1)}, f32[16,512]{1,0:T(8,128)S(1)}, f32[512,16,128]{0,2,1:T(8,128)}, s32[512]{0:T(512)S(1)}, /*index=5*/s...) while((s32[]{:T(128)}, f32[16,512]{1,0:T(8,128)S(1)}, ...), condition=%wide.region_5.6_spmd.clone, body=%wide.region_2.5_spmd.clone.sunk | while | flops 2721891328 | bytes 117522640 | solution.py:128
  116.8 0.3 compare_and_fusion.2
  117.1 4.9 %constant_dynamic-slice_fusion.3 = (bf16[512,2048]{1,0:T(8,128)(2,1)}, bf16[512,2048]{1,0:T(8,128)(2,1)}) fusion(bf16[1024,2048]{1,0:T(8,128)(2,1)} %get-tuple-element.540, s32[]{:T(128)S(6)} %select_n.64, bf16[1024,2048]{1,0:T(8,128)(2,1)} %get-tuple-element.536), kind=kLoop, calls=%fused_computation.22.clone.1 | loop fusion | bytes 8388612 | tf_op jit(solution)/shard_map/while/body/eval_jaxpr/while/body/eval_jaxpr/dynamic_slice | solution.py:95
  122.0 2.9 %copy.58 = bf16[512,2048]{0,1:T(8,128)(2,1)S(1)} copy(bf16[512,2048]{1,0:T(8,128)(2,1)} %get-tuple-element.492) | data formatting | bytes 4194304 | tf_op jit(solution)/shard_map/while/body/eval_jaxpr/while/body/eval_jaxpr/dynamic_slice | solution.py:91
  124.8 4.0 %fusion.43 = f32[16,512,512]{2,1,0:T(8,128)S(1)} fusion(bf16[512,16,128]{0,2,1:T(8,128)(2,1)S(1)} %bitcast.64, bf16[512,16,128]{2,0,1:T(8,128)(2,1)} %get-tuple-element.537), kind=kOutput, calls=%fused_computation.44.clone.1 | convolution fusion | flops 1073741824 | bytes 20971520 | tf_op jit(solution)/shard_map/while/body/eval_jaxpr/while/body/eval_jaxpr/ihd,jhd->hij/dot_general | solution.py:100
  128.8 9.0 %fusion.44 = (f32[16,512]{1,0:T(8,128)S(1)}, f32[16,512,512]{1,2,0:T(8,128)}) fusion(bf16[512,16,64]{0,2,1:T(8,128)(2,1)} %get-tuple-element.539, bf16[1024,64]{0,1:T(8,128)(2,1)S(1)} %get-tuple-element.538, s32[]{:T(128)S(6)} %select_n.64, f32[16,512,512]{2,1,0:T(8,128)S(1)} %fusion.43, pred[512,512]{0,1:T(8,128)(4,1)S(1)} %compare_and_fusion.2), kind=kOutput, calls=%fused_computation.43.clone.1 | convolution fusion | flops 553639936 | bytes 34963460 | tf_op jit(solution)/shard_map/while/body/eval_jaxpr/while/body/eval_jaxpr/ihd,jd->hij/dot_general | solution.py:103
  137.8 2.9 %copy.59 = bf16[512,2048]{0,1:T(8,128)(2,1)S(1)} copy(bf16[512,2048]{1,0:T(8,128)(2,1)} %get-tuple-element.498) | data formatting | bytes 4194304 | tf_op jit(solution)/shard_map/while/body/eval_jaxpr/while/body/eval_jaxpr/dynamic_slice | solution.py:95
  140.7 10.8 %bitcast_add_fusion.3 = f32[512,16,128]{0,2,1:T(8,128)} fusion(f32[512,16,128]{0,2,1:T(8,128)} %get-tuple-element.518, bf16[512,16,128]{0,2,1:T(8,128)(2,1)S(1)} %bitcast.63, f32[16,512,512]{1,2,0:T(8,128)} %get-tuple-element.497, f32[16,512]{1,0:T(8,128)S(1)} %get-tuple-element.531, f32[512,16]{0,1:T(8,128)S(1)} %get-tuple-element.499, ...), kind=kOutput, calls=%fused_computation.10.clone.1 | convolution fusion | flops 1085276160 | bytes 27328512 | tf_op jit(solution)/shard_map/while/body/eval_jaxpr/while/body/eval_jaxpr/hij,jhd->ihd/dot_general | solution.py:114
  151.5 8.3 %fusion.46 = f32[16,512]{1,0:T(8,128)S(1)} fusion(f32[16,512,512]{1,2,0:T(8,128)} %get-tuple-element.497, f32[16,512]{1,0:T(8,128)S(1)} %get-tuple-element.531), kind=kLoop, calls=%fused_computation.7.clone.1 | loop fusion | flops 8380416 | bytes 16842752 | tf_op jit(solution)/shard_map/while/body/eval_jaxpr/while/body/eval_jaxpr/reduce_sum | solution.py:112
  159.9 0.3 compare_and_fusion.2
  160.2 4.9 %constant_dynamic-slice_fusion.3 = (bf16[512,2048]{1,0:T(8,128)(2,1)}, bf16[512,2048]{1,0:T(8,128)(2,1)}) fusion(bf16[1024,2048]{1,0:T(8,128)(2,1)} %get-tuple-element.540, s32[]{:T(128)S(6)} %select_n.64, bf16[1024,2048]{1,0:T(8,128)(2,1)} %get-tuple-element.536), kind=kLoop, calls=%fused_computation.22.clone.1 | loop fusion | bytes 8388612 | tf_op jit(solution)/shard_map/while/body/eval_jaxpr/while/body/eval_jaxpr/dynamic_slice | solution.py:95
  165.1 2.9 %copy.58 = bf16[512,2048]{0,1:T(8,128)(2,1)S(1)} copy(bf16[512,2048]{1,0:T(8,128)(2,1)} %get-tuple-element.492) | data formatting | bytes 4194304 | tf_op jit(solution)/shard_map/while/body/eval_jaxpr/while/body/eval_jaxpr/dynamic_slice | solution.py:91
  167.9 4.0 %fusion.43 = f32[16,512,512]{2,1,0:T(8,128)S(1)} fusion(bf16[512,16,128]{0,2,1:T(8,128)(2,1)S(1)} %bitcast.64, bf16[512,16,128]{2,0,1:T(8,128)(2,1)} %get-tuple-element.537), kind=kOutput, calls=%fused_computation.44.clone.1 | convolution fusion | flops 1073741824 | bytes 20971520 | tf_op jit(solution)/shard_map/while/body/eval_jaxpr/while/body/eval_jaxpr/ihd,jhd->hij/dot_general | solution.py:100
  171.9 9.0 %fusion.44 = (f32[16,512]{1,0:T(8,128)S(1)}, f32[16,512,512]{1,2,0:T(8,128)}) fusion(bf16[512,16,64]{0,2,1:T(8,128)(2,1)} %get-tuple-element.539, bf16[1024,64]{0,1:T(8,128)(2,1)S(1)} %get-tuple-element.538, s32[]{:T(128)S(6)} %select_n.64, f32[16,512,512]{2,1,0:T(8,128)S(1)} %fusion.43, pred[512,512]{0,1:T(8,128)(4,1)S(1)} %compare_and_fusion.2), kind=kOutput, calls=%fused_computation.43.clone.1 | convolution fusion | flops 553639936 | bytes 34963460 | tf_op jit(solution)/shard_map/while/body/eval_jaxpr/while/body/eval_jaxpr/ihd,jd->hij/dot_general | solution.py:103
  180.9 2.9 %copy.59 = bf16[512,2048]{0,1:T(8,128)(2,1)S(1)} copy(bf16[512,2048]{1,0:T(8,128)(2,1)} %get-tuple-element.498) | data formatting | bytes 4194304 | tf_op jit(solution)/shard_map/while/body/eval_jaxpr/while/body/eval_jaxpr/dynamic_slice | solution.py:95
  183.8 12.0 %bitcast_add_fusion.3 = f32[512,16,128]{0,2,1:T(8,128)} fusion(f32[512,16,128]{0,2,1:T(8,128)} %get-tuple-element.518, bf16[512,16,128]{0,2,1:T(8,128)(2,1)S(1)} %bitcast.63, f32[16,512,512]{1,2,0:T(8,128)} %get-tuple-element.497, f32[16,512]{1,0:T(8,128)S(1)} %get-tuple-element.531, f32[512,16]{0,1:T(8,128)S(1)} %get-tuple-element.499, ...), kind=kOutput, calls=%fused_computation.10.clone.1 | convolution fusion | flops 1085276160 | bytes 27328512 | tf_op jit(solution)/shard_map/while/body/eval_jaxpr/while/body/eval_jaxpr/hij,jhd->ihd/dot_general | solution.py:114
  195.8 8.3 %fusion.46 = f32[16,512]{1,0:T(8,128)S(1)} fusion(f32[16,512,512]{1,2,0:T(8,128)} %get-tuple-element.497, f32[16,512]{1,0:T(8,128)S(1)} %get-tuple-element.531), kind=kLoop, calls=%fused_computation.7.clone.1 | loop fusion | flops 8380416 | bytes 16842752 | tf_op jit(solution)/shard_map/while/body/eval_jaxpr/while/body/eval_jaxpr/reduce_sum | solution.py:112
  204.1 2.8 %divide_convert_fusion = bf16[512,16,128]{0,2,1:T(8,128)(2,1)S(1)} fusion(f32[512,16,128]{0,2,1:T(8,128)} %get-tuple-element.292, f32[512,16]{0,1:T(8,128)S(1)} %bitcast.68), kind=kLoop, calls=%fused_computation.25 | loop fusion | flops 2097152 | bytes 6324224 | tf_op jit(solution)/shard_map/while/body/eval_jaxpr/convert_element_type | solution.py:130
  206.9 2.0 reshape.197
  208.9 3.0 %copy.53 = bf16[4,128,2048]{2,1,0:T(8,128)(2,1)S(1)} copy(bf16[4,128,2048]{1,0,2:T(4,128)(2,1)} %reshape.197) | data formatting | bytes 4194304 | tf_op jit(solution)/shard_map/while/body/eval_jaxpr/convert_element_type | solution.py:130
  211.9 28.9 %all_to_all.31 = bf16[4,128,2048]{2,1,0:T(8,128)(2,1)} all-to-all(bf16[4,128,2048]{2,1,0:T(8,128)(2,1)S(1)} %copy.53), channel_id=1, replica_groups=mesh['seq'=8,'head'=4] {'head'}, dimensions={0} | all-to-all | bytes 4194304 | tf_op jit(solution)/shard_map/all_to_all | solution.py:134
  240.8 3.0 %copy.49 = bf16[4,128,2048]{1,2,0:T(8,128)(2,1)S(1)} copy(bf16[4,128,2048]{2,1,0:T(8,128)(2,1)} %all_to_all.31) | data formatting | bytes 4194304 | tf_op jit(solution)/shard_map/all_to_all | solution.py:134
  243.8 2.9 %copy.50 = bf16[128,8192]{1,0:T(8,128)(2,1)} copy(bf16[128,8192]{0,1:T(8,128)(2,1)S(1)} %bitcast.67) | data formatting | bytes 4194304 | tf_op jit(solution)/shard_map/all_to_all | solution.py:134
  (36 shorter events, 0.4 us)
Async XLA Ops:
  6.5 95.4 %all-gather.5.cloned.1.call-start = ((), (), s32[]{:S(2)}) async-start(), calls=%async_computation.3 | async-start | bytes 2359296 | tf_op jit(solution)/shard_map/all_gather | solution.py:71
  7.3 103.4 %all-gather.3.cloned.1.call-start = ((), (), s32[]{:S(2)}) async-start(), calls=%async_computation.2 | async-start | bytes 2359296 | tf_op jit(solution)/shard_map/all_gather | solution.py:66
  12.6 3.9 %copy-start.1 = (bf16[128,512]{1,0:T(8,128)(2,1)S(1)}, bf16[128,512]{1,0:T(8,128)(2,1)}, u32[]{:S(2)}) copy-start(bf16[128,512]{1,0:T(8,128)(2,1)} %param.9) | copy-start | bytes 393220
  12.6 42.1 %copy-start.2 = (bf16[128,64]{0,1:T(8,128)(2,1)S(1)}, bf16[128,64]{0,1:T(8,128)(2,1)}, u32[]{:S(2)}) copy-start(bf16[128,64]{0,1:T(8,128)(2,1)} %param.10) | copy-start | bytes 49156
  12.7 51.2 %copy-start.3 = (s32[32]{0:T(128)S(1)}, s32[32]{0:T(128)}, u32[]{:S(2)}) copy-start(s32[32]{0:T(128)} %param.13) | copy-start | bytes 388
  12.7 63.0 %all-to-all-start = ((bf16[128,4,3072]{0,2,1:T(8,128)(2,1)}), bf16[128,4,3072]{0,2,1:T(8,128)(2,1)S(1)}, u32[]{:S(2)}, u32[]{:S(2)}) async-start(bf16[128,4,3072]{0,2,1:T(8,128)(2,1)} %bitcast.66), calls=%async_computation | async-start | bytes 6291456 | tf_op jit(solution)/shard_map/all_to_all | solution.py:60
  16.5 38.3 %collective-permute-start = (bf16[128,512]{1,0:T(8,128)(2,1)S(1)}, bf16[128,512]{1,0:T(8,128)(2,1)S(1)}, u32[]{:S(2)}, u32[]{:S(2)}) collective-permute-start(bf16[128,512]{1,0:T(8,128)(2,1)S(1)} %copy-done.1), channel_id=1, source_target_pairs={{0,1},{1,2},{2,3},{3,0},{4,5},{5,6},{6,7},{7,4},{8,9},{9,10},{10,1... | collective-permute-start | bytes 393224 | tf_op jit(solution)/shard_map/ppermute | solution.py:27
  54.8 8.9 %collective-permute-start.1 = (bf16[128,512]{1,0:T(8,128)(2,1)S(1)}, bf16[128,512]{1,0:T(8,128)(2,1)}, u32[]{:S(2)}, u32[]{:S(2)}) collective-permute-start(bf16[128,512]{1,0:T(8,128)(2,1)S(1)} %collective-permute-done), channel_id=1, source_target_pairs={{0,1},{1,2},{2,3},{3,0},{4,5},{5,6},{6,7},{7,4},{8,9},{9,10},{10,1... | collective-permute-start | bytes 393224 | tf_op jit(solution)/shard_map/ppermute | solution.py:27
  60.3 14.5 %collective-permute-start.4 = (bf16[512,64]{0,1:T(8,128)(2,1)S(1)}, bf16[512,64]{0,1:T(8,128)(2,1)}, u32[]{:S(2)}, u32[]{:S(2)}) collective-permute-start(bf16[512,64]{0,1:T(8,128)(2,1)S(1)} %all_gather.10), channel_id=1, source_target_pairs={{0,4},{4,8},{8,12},{12,16},{16,20},{20,24},{24,28},{1,5},{5,9},{9,... | collective-permute-start | bytes 196616 | tf_op jit(solution)/shard_map/ppermute | solution.py:37
  63.7 4.8 %collective-permute-start.2 = (bf16[128,512]{1,0:T(8,128)(2,1)}, bf16[128,512]{1,0:T(8,128)(2,1)}, u32[]{:S(2)}, u32[]{:S(2)}) collective-permute-start(bf16[128,512]{1,0:T(8,128)(2,1)} %collective-permute-done.1), channel_id=1, source_target_pairs={{0,1},{1,2},{2,3},{3,0},{4,5},{5,6},{6,7},{7,4},{8,9},{9,10},{10,1... | collective-permute-start | bytes 393224 | tf_op jit(solution)/shard_map/ppermute | solution.py:27
  72.7 29.2 %collective-permute-start.3 = (bf16[512,512]{1,0:T(8,128)(2,1)}, bf16[512,512]{1,0:T(8,128)(2,1)}, u32[]{:S(2)}, u32[]{:S(2)}) collective-permute-start(bf16[512,512]{1,0:T(8,128)(2,1)} %bitcast.69), channel_id=1, source_target_pairs={{0,4},{4,8},{8,12},{12,16},{16,20},{20,24},{24,28},{1,5},{5,9},{9,... | collective-permute-start | bytes 1572872 | tf_op jit(solution)/shard_map/ppermute | solution.py:37
  97.9 4.0 %copy-start = (bf16[4,128,512]{2,1,0:T(8,128)(2,1)S(1)}, bf16[4,128,512]{2,1,0:T(8,128)(2,1)}, u32[]{:S(2)}) copy-start(bf16[4,128,512]{2,1,0:T(8,128)(2,1)} %gather_fusion) | copy-start | bytes 1572868
Sparse Core Ops, SparseCore 0:
  9.5 48.5 all-gather.4
  60.2 50.4 all-gather.2
